TPU v7x, 32 devices: a whole 2x2x4 slice. The times are simulated.
32 devices in a mesh: seq: 16 (over z, x, core), head: 2 (over y).
Axes of the slice: x: 2, y: 2, z: 4, core: 2. Of those that a mesh axis runs over, the one named last changes fastest.
Arguments:
- tokens: bfloat16 [8192, 1024], P('seq'), may hold values from -6 to 6
- mem_query_w: bfloat16 [1024, 1024], P(None, 'head'), may hold values from -0.1875 to 0.1875
- mem_key_w: bfloat16 [1024, 1024], P(None, 'head'), may hold values from -0.1875 to 0.1875
- mem_value_w: bfloat16 [1024, 1024], P(None, 'head'), may hold values from -0.1875 to 0.1875
- mem_in: float32 [1024, 1024], P(None, 'head'), may hold values from -0.1875 to 0.1875
- mem_out: float32 [1024, 1024], P('head'), may hold values from -0.1875 to 0.1875
- forget_levels: float32 [16, 1024], P(None, 'head'), may hold values from 0.003 to 0.3
- momentum_levels: float32 [16, 1024], P(None, 'head'), may hold values from 0.2 to 0.9
- step_levels: float32 [16, 1024], P(None, 'head'), may hold values from 0.02 to 0.2
- plan: int32 [16], P('seq'), may hold values from 0 to 15
- norm_gain: float32 [1024], replicated, may hold values from 0.5 to 1.5
- attn_query_w: bfloat16 [1024, 1024], P(None, 'head'), may hold values from -1 to 1
- attn_key_w: bfloat16 [1024, 1024], P(None, 'head'), may hold values from -4 to 4
- attn_value_w: bfloat16 [1024, 1024], P(None, 'head'), may hold values from -0.1875 to 0.1875
- attn_out_w: bfloat16 [1024, 1024], P('head'), may hold values from -0.25 to 0.25
Outputs:
- layer_out: bfloat16 [8192, 1024], P('seq', 'head')
All inputs are finite; a program needn't handle non-finite values.
Results may differ from a plain program's by a relative error of at most 0.014.
Values may be sent and summed in bfloat16 or wider, within the bound.
A program may use at most 192 MiB of HBM per device.

v0:
```python
import jax
import jax.numpy as jnp
from jax import lax
from jax.sharding import PartitionSpec as P

HEAD_DIM = 64
SPAN = 8


highest = lax.Precision.HIGHEST
epsilon = 1e-06


def entering_2(part, axis, combine, identity):
    place = lax.axis_index(axis)
    gathered = jax.tree.map(lambda a: lax.all_gather(a, axis), part)
    state = jax.tree.map(lambda a, e: jnp.zeros_like(a) + jnp.asarray(e, a.dtype), part, identity)

    def one(lap, state):
        return combine(
            state, jax.tree.map(lambda a: lax.dynamic_index_in_dim(a, lap, 0, False), gathered)
        )

    return lax.fori_loop(0, place, one, state)


def shifted(value, axis, by):
    length = lax.axis_size(axis)
    pairs = [(i, i + by) for i in range(length) if 0 <= i + by < length]
    return lax.ppermute(value, axis, pairs)


def silu_slope(values):
    sigmoid = jax.nn.sigmoid(values)
    return sigmoid * (1.0 + values * (1.0 - sigmoid))


def project(left, weight):
    return jnp.dot(left, weight, preferred_element_type=jnp.float32).astype(jnp.bfloat16)


def normalize(retrieved, norm_gain):
    mean_square = jnp.mean(retrieved * retrieved, axis=-1, keepdims=True)
    return (retrieved * lax.rsqrt(mean_square + epsilon) * norm_gain).astype(jnp.bfloat16)


def lookup(table, chosen):
    matches = jnp.arange(table.shape[0], dtype=jnp.int32)[:, None] == chosen
    return jnp.sum(jnp.where(matches, table, 0.0), axis=0)


def as_columns(vector):
    return vector[..., None, :]


def as_rows(vector):
    return vector[..., :, None]


def compose(earlier, later):
    (
        prior_decay,
        prior_cross,
        prior_keep,
        prior_speed_in,
        prior_speed_out,
        prior_weight_in,
        prior_weight_out,
    ) = earlier
    (
        after_decay,
        after_cross,
        after_keep,
        after_speed_in,
        after_speed_out,
        after_weight_in,
        after_weight_out,
    ) = later
    decay = after_decay * prior_decay
    cross = after_cross * prior_decay + after_keep * prior_cross
    keep = after_keep * prior_keep
    speed_in = as_columns(after_decay) * prior_speed_in + after_speed_in
    speed_out = as_rows(after_decay) * prior_speed_out + after_speed_out
    weight_in = (
        as_columns(after_cross) * prior_speed_in
        + as_columns(after_keep) * prior_weight_in
        + after_weight_in
    )
    weight_out = (
        as_rows(after_cross) * prior_speed_out
        + as_rows(after_keep) * prior_weight_out
        + after_weight_out
    )
    return (decay, cross, keep, speed_in, speed_out, weight_in, weight_out)


def window_attend(query, keys, values, block_index):
    query_count = query.shape[0]
    key_count = keys.shape[0]
    span_rows = key_count - query_count
    distance = (
        span_rows
        + jnp.arange(query_count, dtype=jnp.int32)[:, None]
        - jnp.arange(key_count, dtype=jnp.int32)[None, :]
    )
    key_pos = (block_index * query_count - span_rows + jnp.arange(key_count, dtype=jnp.int32))[
        None, :
    ]
    allowed = (distance >= 0) & (distance < span_rows) & (key_pos >= 0)
    contexts = []
    for head_number in range(query.shape[1] // HEAD_DIM):
        low_col = head_number * HEAD_DIM
        scores = jnp.einsum(
            "qd,kd->qk",
            query[:, low_col : low_col + HEAD_DIM],
            keys[:, low_col : low_col + HEAD_DIM],
            preferred_element_type=jnp.float32,
        ) * HEAD_DIM ** (-0.5)
        scores = jnp.where(allowed, scores, -1e30)
        row_peak = jnp.max(scores, axis=-1, keepdims=True)
        weights = jnp.exp(scores - row_peak)
        probabilities = (weights / jnp.sum(weights, axis=-1, keepdims=True)).astype(jnp.bfloat16)
        contexts.append(
            jnp.dot(
                probabilities,
                values[:, low_col : low_col + HEAD_DIM],
                preferred_element_type=jnp.float32,
            ).astype(jnp.bfloat16)
        )
    return jnp.concatenate(contexts, axis=1)


def shards(
    tokens,
    mem_query_w,
    mem_key_w,
    mem_value_w,
    mem_in,
    mem_out,
    forget_levels,
    momentum_levels,
    step_levels,
    plan,
    norm_gain,
    attn_query_w,
    attn_key_w,
    attn_value_w,
    attn_out_w,
):
    tok_rows = tokens.shape[0]
    share_rows = tok_rows // lax.axis_size("head")
    my_start = lax.axis_index("head") * share_rows
    mem_query, mem_key, mem_value = (
        lax.all_gather(project(tokens, mem_query_w), "head", axis=1, tiled=True),
        lax.all_gather(project(tokens, mem_key_w), "head", axis=1, tiled=True),
        lax.all_gather(project(tokens, mem_value_w), "head", axis=1, tiled=True),
    )
    keys_wide = mem_key.astype(jnp.float32)
    pre_act = jnp.dot(keys_wide, mem_in, precision=highest)
    hidden = jax.nn.silu(pre_act)
    predicted = lax.psum_scatter(
        jnp.dot(hidden, mem_out, precision=highest), "head", scatter_dimension=0, tiled=True
    )
    value_share = lax.dynamic_slice_in_dim(mem_value, my_start, share_rows, 0).astype(jnp.float32)
    residual_err = lax.all_gather(
        2.0 / tok_rows * (predicted - value_share), "head", axis=0, tiled=True
    )
    grad_out = jnp.dot(hidden.T, residual_err, precision=highest)
    slope_term = jnp.dot(residual_err, mem_out.T, precision=highest) * silu_slope(pre_act)
    grad_in = jnp.dot(keys_wide.T, slope_term, precision=highest)
    chosen = plan[0]
    forget = lookup(forget_levels, chosen)
    momentum = lookup(momentum_levels, chosen)
    step_rate = lookup(step_levels, chosen)
    change_in = -as_columns(step_rate) * grad_in
    change_out = -as_rows(step_rate) * grad_out
    element = (momentum, momentum, 1.0 - forget, change_in, change_out, change_in, change_out)
    identity = (
        jnp.ones_like(momentum),
        jnp.zeros_like(momentum),
        jnp.ones_like(momentum),
        jnp.zeros_like(grad_in),
        jnp.zeros_like(grad_out),
        jnp.zeros_like(grad_in),
        jnp.zeros_like(grad_out),
    )
    entering = entering_2(element, "seq", compose, identity)
    weight_in = as_columns(entering[2]) * mem_in + entering[5]
    weight_out = as_rows(entering[2]) * mem_out + entering[6]
    query_hidden = jax.nn.silu(jnp.dot(mem_query.astype(jnp.float32), weight_in, precision=highest))
    retrieved = lax.psum_scatter(
        jnp.dot(query_hidden, weight_out, precision=highest),
        "head",
        scatter_dimension=0,
        tiled=True,
    )
    normed = lax.all_gather(normalize(retrieved, norm_gain), "head", axis=0, tiled=True)
    att_query = project(normed, attn_query_w)
    att_key = project(normed, attn_key_w)
    att_value = project(normed, attn_value_w)
    earlier = []
    for distance in range(SPAN, 0, -1):
        earlier.append(shifted((att_key, att_value), "seq", distance))
    key_window = jnp.concatenate([received[0] for received in earlier] + [att_key], axis=0)
    value_window = jnp.concatenate([received[1] for received in earlier] + [att_value], axis=0)
    context = window_attend(att_query, key_window, value_window, lax.axis_index("seq"))
    partial_out = jnp.dot(context, attn_out_w, preferred_element_type=jnp.float32)
    return lax.psum_scatter(
        partial_out.astype(jnp.bfloat16), "head", scatter_dimension=1, tiled=True
    )


def solution(mesh):
    in_specs = (
        P("seq", None),
        P(None, "head"),
        P(None, "head"),
        P(None, "head"),
        P(None, "head"),
        P("head", None),
        P(None, "head"),
        P(None, "head"),
        P(None, "head"),
        P("seq"),
        P(),
        P(None, "head"),
        P(None, "head"),
        P(None, "head"),
        P("head", None),
    )
    out_specs = P("seq", "head")
    return jax.shard_map(shards, mesh=mesh, in_specs=in_specs, out_specs=out_specs, check_vma=False)
```

profile of v0, /device:TPU:27, one launch (start us, length us, event | category | flops | bytes accessed | tf_op | source)
XLA Modules:
  0.0 1014.6 jit_solution(4729358070091135776)
XLA Ops:
  13.4 19.4 %all-gather.16.cloned.1.call-done = bf16[512,1024]{1,0:T(8,128)(2,1)} async-done(((bf16[512,512]{1,0:T(8,128)(2,1)}), bf16[512,1024]{1,0:T(8,128)(2,1)}) %all-gather.16.cloned.1.call-update) | async-done | bytes 1048592 | tf_op jit(solution)/shard_map/all_gather | solution.py:155
  36.8 6.6 fusion.76
  43.5 12.1 %all-gather.18.cloned.1.call-done = bf16[512,1024]{1,0:T(8,128)(2,1)} async-done(((bf16[512,512]{1,0:T(8,128)(2,1)}), bf16[512,1024]{1,0:T(8,128)(2,1)}) %all-gather.18.cloned.1.call-update) | async-done | bytes 1048592 | tf_op jit(solution)/shard_map/all_gather | solution.py:156
  55.6 34.2 %reduce-scatter.4.cloned.1.call-done = f32[256,1024]{1,0:T(8,128)} async-done(((f32[512,1024]{1,0:T(8,128)}), f32[256,1024]{1,0:T(8,128)}) %reduce-scatter.4.cloned.1.call-update) | async-done | bytes 1048592 | tf_op jit(solution)/shard_map/reduce_scatter | solution.py:161
  93.7 31.9 %all-gather.20.cloned.1.call-done = f32[512,1024]{1,0:T(8,128)} async-done(((f32[256,1024]{1,0:T(8,128)}), f32[512,1024]{1,0:T(8,128)}) %all-gather.20.cloned.1.call-update) | async-done | bytes 2097168 | tf_op jit(solution)/shard_map/all_gather | solution.py:165
  125.6 5.9 convolution_multiply_fusion.2
  134.9 6.6 convolution_multiply_fusion.1
  143.2 17.6 %all-gather.4 = f32[16,1,512]{2,1,0:T(1,128)S(1)} all-gather(f32[1,1,512]{2,1,0:T(1,128)S(1)} %bitcast.73), channel_id=2, replica_groups=mesh['seq'=16,'head'=2] {'seq'}, dimensions={0}, use_global_device_ids=true | all-gather | bytes 34816 | tf_op jit(solution)/shard_map/all_gather | solution.py:16
  160.8 20.8 %all-gather.5 = f32[16,1,512]{2,1,0:T(1,128)S(1)} all-gather(f32[1,1,512]{2,1,0:T(1,128)S(1)} %bitcast.72), channel_id=3, replica_groups=mesh['seq'=16,'head'=2] {'seq'}, dimensions={0}, use_global_device_ids=true | all-gather | bytes 34816 | tf_op jit(solution)/shard_map/all_gather | solution.py:16
  181.6 121.5 %all-gather.24.cloned.1.call-done = f32[16384,512]{1,0:T(8,128)} async-done(((f32[1024,512]{1,0:T(8,128)}), f32[16384,512]{1,0:T(8,128)}) %all-gather.24.cloned.1.call-update) | async-done | bytes 33554448 | tf_op jit(solution)/shard_map/all_gather | solution.py:16
  303.0 169.8 %all-gather.26.cloned.1.call-done = f32[8192,1024]{1,0:T(8,128)} async-done(((f32[512,1024]{1,0:T(8,128)}), f32[8192,1024]{1,0:T(8,128)}) %all-gather.26.cloned.1.call-update) | async-done | bytes 33554448 | tf_op jit(solution)/shard_map/all_gather | solution.py:16
  477.9 152.6 %while.22 = (s32[]{:T(128)}, f32[512]{0:T(512)S(1)}, f32[1024,512]{1,0:T(8,128)}, f32[512,1024]{1,0:T(8,128)}, f32[1024,512]{1,0:T(8,128)S(1)}, /*index=5*/f32[5...) while((s32[]{:T(128)}, f32[512]{0:T(512)S(1)}, ...), condition=%wide.region_5.6_spmd, body=%wide.region_4.5_spmd.sunk | while | flops 5243397 | bytes 37771496 | solution.py:24
  640.0 32.2 %reduce-scatter.6.cloned.1.call-done = f32[256,1024]{1,0:T(8,128)} async-done(((f32[512,1024]{1,0:T(8,128)}), f32[256,1024]{1,0:T(8,128)}) %reduce-scatter.6.cloned.1.call-update) | async-done | bytes 1048592 | tf_op jit(solution)/shard_map/reduce_scatter | solution.py:191
  675.9 21.4 %all-gather.22.cloned.1.call-done = bf16[512,1024]{1,0:T(8,128)(2,1)} async-done(((bf16[256,1024]{1,0:T(8,128)(2,1)}), bf16[512,1024]{1,0:T(8,128)(2,1)}) %all-gather.22.cloned.1.call-update) | async-done | bytes 1048592 | tf_op jit(solution)/shard_map/all_gather | solution.py:197
  709.8 45.5 %collective-permute-done = bf16[512,512]{1,0:T(8,128)(2,1)S(1)} collective-permute-done((bf16[512,512]{1,0:T(8,128)(2,1)S(1)}, bf16[512,512]{1,0:T(8,128)(2,1)S(1)}, u32[]{:S(2)}, u32[]{:S(2)}) %collective-permute-start) | collective-permute-done | bytes 524320 | tf_op jit(solution)/shard_map/ppermute | solution.py:30
  767.4 13.4 %collective-permute-done.6 = bf16[512,512]{1,0:T(8,128)(2,1)S(1)} collective-permute-done((bf16[512,512]{1,0:T(8,128)(2,1)S(1)}, bf16[512,512]{1,0:T(8,128)(2,1)S(1)}, u32[]{:S(2)}, u32[]{:S(2)}) %collective-permute-start.6) | collective-permute-done | bytes 524320 | tf_op jit(solution)/shard_map/ppermute | solution.py:30
  788.0 96.3 %collective-permute-done.8 = bf16[512,512]{1,0:T(8,128)(2,1)S(1)} collective-permute-done((bf16[512,512]{1,0:T(8,128)(2,1)S(1)}, bf16[512,512]{1,0:T(8,128)(2,1)S(1)}, u32[]{:S(2)}, u32[]{:S(2)}) %collective-permute-start.8) | collective-permute-done | bytes 524320 | tf_op jit(solution)/shard_map/ppermute | solution.py:30
  891.3 6.6 fusion.94
  899.7 6.8 fusion.93
  906.5 6.7 fusion.92
  913.2 6.7 fusion.91
  920.0 6.6 fusion.90
  926.6 6.8 fusion.89
  967.5 40.0 %reduce-scatter.8.cloned.1.call-done = bf16[512,512]{1,0:T(8,128)(2,1)} async-done(((bf16[512,1024]{1,0:T(8,128)(2,1)}), bf16[512,512]{1,0:T(8,128)(2,1)}) %reduce-scatter.8.cloned.1.call-update) | async-done | bytes 524304 | tf_op jit(solution)/shard_map/reduce_scatter | solution.py:208
  (309 shorter events, 263.6 us)
Async XLA Ops:
  6.5 26.2 %all-gather.16.cloned.1.call-start = ((), (), s32[]{:S(2)}) async-start(), calls=%async_computation.4 | async-start | bytes 1572864 | tf_op jit(solution)/shard_map/all_gather | solution.py:155
  10.5 45.1 %all-gather.18.cloned.1.call-start = ((), (), s32[]{:S(2)}) async-start(), calls=%async_computation.6 | async-start | bytes 1572864 | tf_op jit(solution)/shard_map/all_gather | solution.py:156
  13.3 76.5 %reduce-scatter.4.cloned.1.call-start = ((), (), s32[]{:S(2)}) async-start(), calls=%async_computation.5 | async-start | bytes 3145728 | tf_op jit(solution)/shard_map/reduce_scatter | solution.py:161
  43.4 82.1 %all-gather.20.cloned.1.call-start = ((), (), s32[]{:S(2)}) async-start(), calls=%async_computation.7 | async-start | bytes 3145728 | tf_op jit(solution)/shard_map/all_gather | solution.py:165
  92.3 210.7 %all-gather.24.cloned.1.call-start = ((), (), s32[]{:S(2)}) async-start(), calls=%async_computation.11 | async-start | bytes 35651584 | tf_op jit(solution)/shard_map/all_gather | solution.py:16
  134.9 337.9 %all-gather.26.cloned.1.call-start = ((), (), s32[]{:S(2)}) async-start(), calls=%async_computation.12 | async-start | bytes 35651584 | tf_op jit(solution)/shard_map/all_gather | solution.py:16
  141.5 489.1 %all-gather.14.cloned.1.call-start = ((), (), s32[]{:S(2)}) async-start(), calls=%async_computation.3 | async-start | bytes 1572864 | tf_op jit(solution)/shard_map/all_gather | solution.py:154
  143.1 529.1 %reduce-scatter.6.cloned.1.call-start = ((), (), s32[]{:S(2)}) async-start(), calls=%async_computation.8 | async-start | bytes 3145728 | tf_op jit(solution)/shard_map/reduce_scatter | solution.py:191
  640.0 57.3 %all-gather.22.cloned.1.call-start = ((), (), s32[]{:S(2)}) async-start(), calls=%async_computation.9 | async-start | bytes 1572864 | tf_op jit(solution)/shard_map/all_gather | solution.py:197
  675.8 331.7 %reduce-scatter.8.cloned.1.call-start = ((), (), s32[]{:S(2)}) async-start(), calls=%async_computation.10 | async-start | bytes 1572864 | tf_op jit(solution)/shard_map/reduce_scatter | solution.py:208
  699.3 55.9 %collective-permute-start = (bf16[512,512]{1,0:T(8,128)(2,1)S(1)}, bf16[512,512]{1,0:T(8,128)(2,1)S(1)}, u32[]{:S(2)}, u32[]{:S(2)}) collective-permute-start(bf16[512,512]{1,0:T(8,128)(2,1)S(1)} %convolution_convert_fusion.2), channel_id=1, source_target_pairs={{0,16},{2,18},{4,20},{6,22},{8,24},{10,26},{12,28},{14,30},{1,17},... | collective-permute-start | bytes 1572872 | tf_op jit(solution)/shard_map/ppermute | solution.py:30
  700.6 56.0 %collective-permute-start.1 = (bf16[512,512]{1,0:T(8,128)(2,1)S(1)}, bf16[512,512]{1,0:T(8,128)(2,1)S(1)}, u32[]{:S(2)}, u32[]{:S(2)}) collective-permute-start(bf16[512,512]{1,0:T(8,128)(2,1)S(1)} %convolution_convert_fusion.2), channel_id=1, source_target_pairs={{0,14},{2,16},{4,18},{6,20},{8,22},{10,24},{12,26},{14,28},{16,30}... | collective-permute-start | bytes 1572872 | tf_op jit(solution)/shard_map/ppermute | solution.py:30
  701.9 56.0 %collective-permute-start.2 = (bf16[512,512]{1,0:T(8,128)(2,1)S(1)}, bf16[512,512]{1,0:T(8,128)(2,1)S(1)}, u32[]{:S(2)}, u32[]{:S(2)}) collective-permute-start(bf16[512,512]{1,0:T(8,128)(2,1)S(1)} %convolution_convert_fusion.2), channel_id=1, source_target_pairs={{0,12},{2,14},{4,16},{6,18},{8,20},{10,22},{12,24},{14,26},{16,28}... | collective-permute-start | bytes 1572872 | tf_op jit(solution)/shard_map/ppermute | solution.py:30
  703.2 56.1 %collective-permute-start.3 = (bf16[512,512]{1,0:T(8,128)(2,1)S(1)}, bf16[512,512]{1,0:T(8,128)(2,1)S(1)}, u32[]{:S(2)}, u32[]{:S(2)}) collective-permute-start(bf16[512,512]{1,0:T(8,128)(2,1)S(1)} %convolution_convert_fusion.2), channel_id=1, source_target_pairs={{0,10},{2,12},{4,14},{6,16},{8,18},{10,20},{12,22},{14,24},{16,26}... | collective-permute-start | bytes 1572872 | tf_op jit(solution)/shard_map/ppermute | solution.py:30
  704.5 56.1 %collective-permute-start.4 = (bf16[512,512]{1,0:T(8,128)(2,1)S(1)}, bf16[512,512]{1,0:T(8,128)(2,1)S(1)}, u32[]{:S(2)}, u32[]{:S(2)}) collective-permute-start(bf16[512,512]{1,0:T(8,128)(2,1)S(1)} %convolution_convert_fusion.2), channel_id=1, source_target_pairs={{0,8},{2,10},{4,12},{6,14},{8,16},{10,18},{12,20},{14,22},{16,24},... | collective-permute-start | bytes 1572872 | tf_op jit(solution)/shard_map/ppermute | solution.py:30
  756.6 24.2 %collective-permute-start.6 = (bf16[512,512]{1,0:T(8,128)(2,1)S(1)}, bf16[512,512]{1,0:T(8,128)(2,1)S(1)}, u32[]{:S(2)}, u32[]{:S(2)}) collective-permute-start(bf16[512,512]{1,0:T(8,128)(2,1)S(1)} %convolution_convert_fusion.2), channel_id=1, source_target_pairs={{0,4},{2,6},{4,8},{6,10},{8,12},{10,14},{12,16},{14,18},{16,20},{1... | collective-permute-start | bytes 1572872 | tf_op jit(solution)/shard_map/ppermute | solution.py:30
  759.3 125.0 %collective-permute-start.8 = (bf16[512,512]{1,0:T(8,128)(2,1)S(1)}, bf16[512,512]{1,0:T(8,128)(2,1)S(1)}, u32[]{:S(2)}, u32[]{:S(2)}) collective-permute-start(bf16[512,512]{1,0:T(8,128)(2,1)S(1)} %convolution_convert_fusion.1), channel_id=1, source_target_pairs={{0,16},{2,18},{4,20},{6,22},{8,24},{10,26},{12,28},{14,30},{1,17},... | collective-permute-start | bytes 1572872 | tf_op jit(solution)/shard_map/ppermute | solution.py:30
  760.7 129.3 %collective-permute-start.9 = (bf16[512,512]{1,0:T(8,128)(2,1)S(1)}, bf16[512,512]{1,0:T(8,128)(2,1)S(1)}, u32[]{:S(2)}, u32[]{:S(2)}) collective-permute-start(bf16[512,512]{1,0:T(8,128)(2,1)S(1)} %convolution_convert_fusion.1), channel_id=1, source_target_pairs={{0,14},{2,16},{4,18},{6,20},{8,22},{10,24},{12,26},{14,28},{16,30}... | collective-permute-start | bytes 1572872 | tf_op jit(solution)/shard_map/ppermute | solution.py:30
  766.0 131.9 %collective-permute-start.10 = (bf16[512,512]{1,0:T(8,128)(2,1)S(1)}, bf16[512,512]{1,0:T(8,128)(2,1)S(1)}, u32[]{:S(2)}, u32[]{:S(2)}) collective-permute-start(bf16[512,512]{1,0:T(8,128)(2,1)S(1)} %convolution_convert_fusion.1), channel_id=1, source_target_pairs={{0,12},{2,14},{4,16},{6,18},{8,20},{10,22},{12,24},{14,26},{16,28}... | collective-permute-start | bytes 1572872 | tf_op jit(solution)/shard_map/ppermute | solution.py:30
  780.8 125.6 %collective-permute-start.11 = (bf16[512,512]{1,0:T(8,128)(2,1)S(1)}, bf16[512,512]{1,0:T(8,128)(2,1)S(1)}, u32[]{:S(2)}, u32[]{:S(2)}) collective-permute-start(bf16[512,512]{1,0:T(8,128)(2,1)S(1)} %convolution_convert_fusion.1), channel_id=1, source_target_pairs={{0,10},{2,12},{4,14},{6,16},{8,18},{10,20},{12,22},{14,24},{16,26}... | collective-permute-start | bytes 1572872 | tf_op jit(solution)/shard_map/ppermute | solution.py:30
  782.2 131.0 %collective-permute-start.12 = (bf16[512,512]{1,0:T(8,128)(2,1)S(1)}, bf16[512,512]{1,0:T(8,128)(2,1)S(1)}, u32[]{:S(2)}, u32[]{:S(2)}) collective-permute-start(bf16[512,512]{1,0:T(8,128)(2,1)S(1)} %convolution_convert_fusion.1), channel_id=1, source_target_pairs={{0,8},{2,10},{4,12},{6,14},{8,16},{10,18},{12,20},{14,22},{16,24},... | collective-permute-start | bytes 1572872 | tf_op jit(solution)/shard_map/ppermute | solution.py:30
  884.3 35.6 %collective-permute-start.13 = (bf16[512,512]{1,0:T(8,128)(2,1)S(1)}, bf16[512,512]{1,0:T(8,128)(2,1)S(1)}, u32[]{:S(2)}, u32[]{:S(2)}) collective-permute-start(bf16[512,512]{1,0:T(8,128)(2,1)S(1)} %convolution_convert_fusion.1), channel_id=1, source_target_pairs={{0,6},{2,8},{4,10},{6,12},{8,14},{10,16},{12,18},{14,20},{16,22},{... | collective-permute-start | bytes 1572872 | tf_op jit(solution)/shard_map/ppermute | solution.py:30
  889.9 36.7 %collective-permute-start.14 = (bf16[512,512]{1,0:T(8,128)(2,1)S(1)}, bf16[512,512]{1,0:T(8,128)(2,1)S(1)}, u32[]{:S(2)}, u32[]{:S(2)}) collective-permute-start(bf16[512,512]{1,0:T(8,128)(2,1)S(1)} %convolution_convert_fusion.1), channel_id=1, source_target_pairs={{0,4},{2,6},{4,8},{6,10},{8,12},{10,14},{12,16},{14,18},{16,20},{1... | collective-permute-start | bytes 1572872 | tf_op jit(solution)/shard_map/ppermute | solution.py:30
  897.9 35.5 %collective-permute-start.15 = (bf16[512,512]{1,0:T(8,128)(2,1)S(1)}, bf16[512,512]{1,0:T(8,128)(2,1)S(1)}, u32[]{:S(2)}, u32[]{:S(2)}) collective-permute-start(bf16[512,512]{1,0:T(8,128)(2,1)S(1)} %convolution_convert_fusion.1), channel_id=1, source_target_pairs={{0,2},{2,4},{4,6},{6,8},{8,10},{10,12},{12,14},{14,16},{16,18},{18... | collective-permute-start | bytes 1572872 | tf_op jit(solution)/shard_map/ppermute | solution.py:30
  (66 other events, 746.1 us)
Sparse Core Ops, SparseCore 0:
  10.6 22.0 all-gather.15
  34.3 21.2 all-gather.17
  57.8 31.8 reduce-scatter.3
  92.5 33.0 all-gather.19
  135.0 168.0 all-gather.23
  304.5 168.2 all-gather.25
  474.3 21.6 all-gather.13
  640.1 32.1 reduce-scatter.5
  676.0 21.2 all-gather.21
  967.6 39.8 reduce-scatter.7
where the time goes:
time: 1020 us; the launch traced here: 1010 us
  waiting for transfers between devices  642 us (63%)
  other arithmetic  149 us (15%)
  matrix products  114 us (11%)
  blocking collectives  38.4 us (4%)
  local copies, waits for them, and re-layouts  34.1 us (3%)
  starting transfers between devices  22.1 us (2%)
  between operations  15.2 us (1%)
    all_gather x2, waiting for transfers between devices, entering_2(): gathered = jax.tree.map(lambda a: lax.all_gather(a, axis), part)  291 us
    ppermute x16, waiting for transfers between devices, shifted(): return lax.ppermute(value, axis, pairs)  159 us
    add x15, other arithmetic, compose(): as_rows(after_cross) * prior_speed_out  83 us
    dot_general x8, matrix products, window_attend(): jnp.einsum('qd,kd->qk', query[:, low_col:low_col + HEAD_DIM], keys[:, low...  48.8 us
    add x15, other arithmetic, compose(): as_columns(after_cross) * prior_speed_in  48.3 us
    reduce_scatter x1, waiting for transfers between devices, shards(): lax.psum_scatter(partial_out.astype(jnp.bfloat16), 'head', scatter_dimens...  40 us
    all_gather x2, blocking collectives, entering_2(): gathered = jax.tree.map(lambda a: lax.all_gather(a, axis), part)  38.4 us
    reduce_scatter x1, waiting for transfers between devices, shards(): lax.psum_scatter(jnp.dot(hidden, mem_out, precision=highest), 'head', sca...  34.2 us
  transfers between devices with their start and end apart: 26, of which 13 were waited for; matrix products, arithmetic and copies ran while one was open for 21% of the time, Pallas kernels for 0%

commit v1 on v0

v1 whole, which is shorter than its diff:
```python
import functools
import math

import jax
import jax.numpy as jnp
from jax import lax
from jax.experimental import pallas as pl
from jax.experimental.pallas import tpu as pltpu
from jax.sharding import PartitionSpec as P

HEAD_DIM = 64
LANES = 2 * HEAD_DIM
SPAN = 8
MESH = pl.DeviceIdType.MESH

epsilon = 1e-06
ANY = pl.BlockSpec(memory_space=pl.ANY)
VMEM = pl.BlockSpec(memory_space=pltpu.VMEM)


def meet(axis, n):
    me = lax.axis_index(axis)
    barrier = pltpu.get_barrier_semaphore()
    for k in range(1, n):
        pl.semaphore_signal(
            barrier, inc=1, device_id={axis: lax.rem(me + k, n)}, device_id_type=MESH
        )
    pl.semaphore_wait(barrier, n - 1)


def remote(src, dst, send, recv, axis, peer):
    return pltpu.make_async_remote_copy(
        src_ref=src,
        dst_ref=dst,
        send_sem=send,
        recv_sem=recv,
        device_id={axis: peer},
        device_id_type=MESH,
    )


def part(ref, dim, index, size):
    window = pl.ds(pl.multiple_of(index * size, size), size)
    return ref.at[:, window] if dim == 1 else ref.at[window, :]


def gather_kernel(axis, n, dim, size, x_ref, o_ref, send, recv, local):
    me = lax.axis_index(axis)
    meet(axis, n)
    slot = part(o_ref, dim, me, size)
    copies = []
    for k in range(1, n):
        copy = remote(x_ref, slot, send.at[k - 1], recv.at[k - 1], axis, lax.rem(me + k, n))
        copy.start()
        copies.append(copy)
    own = pltpu.make_async_copy(x_ref, slot, local)
    own.start()
    own.wait()
    for copy in copies:
        copy.wait()


def split_kernel(axis, n, dim, size, x_ref, o_ref, send, recv, local):
    me = lax.axis_index(axis)
    meet(axis, n)
    copies = []
    for k in range(1, n):
        peer = lax.rem(me + k, n)
        copy = remote(
            part(x_ref, dim, peer, size),
            o_ref.at[me],
            send.at[k - 1],
            recv.at[k - 1],
            axis,
            peer,
        )
        copy.start()
        copies.append(copy)
    own = pltpu.make_async_copy(part(x_ref, dim, me, size), o_ref.at[me], local)
    own.start()
    own.wait()
    for copy in copies:
        copy.wait()


def comm_call(kernel, out, n, identity, x):
    return pl.pallas_call(
        kernel,
        out_shape=out,
        in_specs=[ANY],
        out_specs=ANY,
        scratch_shapes=[
            pltpu.SemaphoreType.DMA((n - 1,)),
            pltpu.SemaphoreType.DMA((n - 1,)),
            pltpu.SemaphoreType.DMA,
        ],
        compiler_params=pltpu.CompilerParams(collective_id=identity, has_side_effects=True),
    )(x)


def gather(x, axis, dim, identity):
    n = lax.axis_size(axis)
    shape = list(x.shape)
    shape[dim] *= n
    kernel = functools.partial(gather_kernel, axis, n, dim, x.shape[dim])
    return comm_call(kernel, jax.ShapeDtypeStruct(tuple(shape), x.dtype), n, identity, x)


def scatter_sum(x, axis, dim, identity):
    n = lax.axis_size(axis)
    shape = list(x.shape)
    shape[dim] //= n
    kernel = functools.partial(split_kernel, axis, n, dim, shape[dim])
    parts = comm_call(kernel, jax.ShapeDtypeStruct((n, *shape), x.dtype), n, identity, x)
    return jnp.sum(parts.astype(jnp.float32), axis=0)


def memory_kernel(
    n, grads_ref, first_ref, forget_ref, momentum_ref, rate_ref, o_ref,
    came, stage, send, recv, send_back, recv_back, local, local_back,
):
    me = lax.axis_index("seq")
    meet("seq", n)
    copies = []
    for k in range(1, n):
        peer = lax.rem(me + k, n)
        copy = remote(
            grads_ref.at[peer], came.at[me], send.at[k - 1], recv.at[k - 1], "seq", peer
        )
        copy.start()
        copies.append(copy)
    own = pltpu.make_async_copy(grads_ref.at[me], came.at[me], local)
    own.start()
    own.wait()
    for copy in copies:
        copy.wait()

    def columns(c, carry):
        window = pl.ds(pl.multiple_of(c * 128, 128), 128)
        weight = first_ref[:, window]
        speed = jnp.zeros_like(weight)
        for g in range(n):
            stage[g, :, window] = weight.astype(jnp.bfloat16)
            if g < n - 1:
                grad = came[g, :, window].astype(jnp.float32)
                speed = momentum_ref[g] * speed - rate_ref[g] * grad
                weight = (1.0 - forget_ref[g]) * weight + speed
        return carry

    lax.fori_loop(0, first_ref.shape[1] // 128, columns, 0)

    copies = []
    for k in range(1, n):
        peer = lax.rem(me + k, n)
        copy = remote(
            stage.at[peer], o_ref.at[me], send_back.at[k - 1], recv_back.at[k - 1], "seq", peer
        )
        copy.start()
        copies.append(copy)
    own = pltpu.make_async_copy(stage.at[me], o_ref.at[me], local_back)
    own.start()
    own.wait()
    for copy in copies:
        copy.wait()


def evolve(grads, first, forget, momentum, rate, identity):
    n = grads.shape[0]
    return pl.pallas_call(
        functools.partial(memory_kernel, n),
        out_shape=jax.ShapeDtypeStruct(grads.shape, jnp.bfloat16),
        in_specs=[ANY, VMEM, VMEM, VMEM, VMEM],
        out_specs=ANY,
        scratch_shapes=[
            pltpu.VMEM(grads.shape, jnp.bfloat16),
            pltpu.VMEM(grads.shape, jnp.bfloat16),
            pltpu.SemaphoreType.DMA((n - 1,)),
            pltpu.SemaphoreType.DMA((n - 1,)),
            pltpu.SemaphoreType.DMA((n - 1,)),
            pltpu.SemaphoreType.DMA((n - 1,)),
            pltpu.SemaphoreType.DMA,
            pltpu.SemaphoreType.DMA,
        ],
        compiler_params=pltpu.CompilerParams(collective_id=identity, has_side_effects=True),
    )(grads, first, forget, momentum, rate)


def attention_kernel(
    n, heads, q_ref, kv_ref, o_ref,
    q_all, kv_all, ctx, q_send, q_recv, kv_send, kv_recv, ctx_send, ctx_recv, local,
):
    me = lax.axis_index("seq")
    chunk = me // heads
    head = lax.rem(me, heads)
    other = lax.rem(me + 1, n)
    rows = q_ref.shape[0]
    slots = SPAN + heads
    first_block = chunk * heads - SPAN
    my_slot = me - first_block
    my_tile = lax.rem(me, heads)

    def lanes(ref, which):
        return ref.at[:, pl.ds(pl.multiple_of(which * LANES, LANES), LANES)]

    def outgoing(k):
        peer = lax.rem(me + k, n)
        peer_chunk = peer // heads
        peer_head = lax.rem(peer, heads)
        slot = me - peer_chunk * heads + SPAN
        wanted = jnp.logical_and(slot >= 0, slot < slots)
        same = peer_chunk == chunk
        safe = jnp.where(wanted, slot, 0)
        kv_copy = remote(
            lanes(kv_ref, peer_head), kv_all.at[safe], kv_send.at[k - 1], kv_recv.at[safe], "seq", peer
        )
        q_copy = remote(
            lanes(q_ref, peer_head), q_all.at[my_tile], q_send.at[k - 1], q_recv.at[my_tile], "seq", peer
        )
        return wanted, same, kv_copy, q_copy

    meet("seq", n)
    own_kv = pltpu.make_async_copy(lanes(kv_ref, head), kv_all.at[my_slot], local.at[0])
    own_q = pltpu.make_async_copy(lanes(q_ref, head), q_all.at[my_tile], local.at[1])
    own_kv.start()
    own_q.start()
    for k in range(1, n):
        wanted, same, kv_copy, q_copy = outgoing(k)

        @pl.when(same)
        def _():
            q_copy.start()

        @pl.when(wanted)
        def _():
            kv_copy.start()

    own_kv.wait()
    own_q.wait()

    def await_kv(slot):
        block = first_block + slot

        @pl.when(jnp.logical_and(block >= 0, block != me))
        def _():
            remote(
                kv_all.at[slot], kv_all.at[slot], kv_send.at[0], kv_recv.at[slot], "seq", other
            ).wait_recv()

    for slot in range(SPAN):
        await_kv(slot)

    row = lax.broadcasted_iota(jnp.int32, (rows, rows), 0)
    column = lax.broadcasted_iota(jnp.int32, (rows, rows), 1)
    scale = math.log2(math.e) * HEAD_DIM**-0.5

    def scored(query, slot):
        pair = kv_all[slot]
        scores = lax.dot_general(
            query, pair, (((1,), (1,)), ((), ())), preferred_element_type=jnp.float32
        ) * scale
        lane = lax.broadcasted_iota(jnp.int32, pair.shape, 1)
        values = jnp.where(lane < HEAD_DIM, jnp.ones_like(pair), pair)
        return scores, values

    def absorb(state, scores, values):
        peak, total = state
        new_peak = jnp.maximum(peak, jnp.max(scores, axis=1, keepdims=True))
        weights = jnp.exp2(scores - new_peak).astype(jnp.bfloat16)
        total = total * jnp.exp2(peak - new_peak) + jnp.dot(
            weights, values, preferred_element_type=jnp.float32
        )
        return new_peak, total

    def returned(tile):
        return remote(
            ctx.at[tile], lanes(o_ref, head), ctx_send.at[tile], ctx_recv.at[head], "seq",
            chunk * heads + tile,
        )

    def one_tile(tile, carry):
        @pl.when(tile != my_tile)
        def _():
            remote(
                q_all.at[tile], q_all.at[tile], q_send.at[0], q_recv.at[tile], "seq", other
            ).wait_recv()

        await_kv(tile + SPAN)
        query = q_all[tile]
        block = chunk * heads + tile
        scores, values = scored(query, tile + SPAN)
        scores = jnp.where(column <= row, scores, -1e30)
        peak = jnp.max(scores, axis=1, keepdims=True)
        weights = jnp.exp2(scores - peak).astype(jnp.bfloat16)
        state = (peak, jnp.dot(weights, values, preferred_element_type=jnp.float32))

        def whole(back, state):
            scores, values = scored(query, tile + SPAN - back)
            return absorb(state, scores, values)

        state = lax.fori_loop(1, jnp.minimum(block, SPAN - 1) + 1, whole, state)

        def oldest(back, state):
            scores, values = scored(query, tile)
            return absorb(state, jnp.where(column > row, scores, -1e30), values)

        peak, total = lax.fori_loop(0, jnp.where(block >= SPAN, 1, 0), oldest, state)
        ctx[tile] = (total / total[:, :1]).astype(jnp.bfloat16)

        @pl.when(tile != my_tile)
        def _():
            returned(tile).start()

        @pl.when(tile == my_tile)
        def _():
            pltpu.make_async_copy(ctx.at[tile], lanes(o_ref, head), local.at[2]).start()

        return carry

    lax.fori_loop(0, heads, one_tile, 0)

    pltpu.make_async_copy(ctx.at[my_tile], lanes(o_ref, head), local.at[2]).wait()
    for tile in range(heads):
        @pl.when(tile != my_tile)
        def _():
            returned(tile).wait_send()
            remote(
                ctx.at[tile], lanes(o_ref, tile), ctx_send.at[tile], ctx_recv.at[tile], "seq", other
            ).wait_recv()

    for k in range(1, n):
        wanted, same, kv_copy, q_copy = outgoing(k)

        @pl.when(same)
        def _():
            q_copy.wait_send()

        @pl.when(wanted)
        def _():
            kv_copy.wait_send()


def attend(query, pairs, identity):
    n = lax.axis_size("seq")
    rows = query.shape[0]
    heads = query.shape[1] // LANES
    return pl.pallas_call(
        functools.partial(attention_kernel, n, heads),
        out_shape=jax.ShapeDtypeStruct(query.shape, jnp.bfloat16),
        in_specs=[ANY, ANY],
        out_specs=ANY,
        scratch_shapes=[
            pltpu.VMEM((heads, rows, LANES), jnp.bfloat16),
            pltpu.VMEM((SPAN + heads, rows, LANES), jnp.bfloat16),
            pltpu.VMEM((heads, rows, LANES), jnp.bfloat16),
            pltpu.SemaphoreType.DMA((n - 1,)),
            pltpu.SemaphoreType.DMA((heads,)),
            pltpu.SemaphoreType.DMA((n - 1,)),
            pltpu.SemaphoreType.DMA((SPAN + heads,)),
            pltpu.SemaphoreType.DMA((heads,)),
            pltpu.SemaphoreType.DMA((heads,)),
            pltpu.SemaphoreType.DMA((3,)),
        ],
        compiler_params=pltpu.CompilerParams(collective_id=identity, has_side_effects=True),
    )(query, pairs)


def silu_slope(values):
    sigmoid = jax.nn.sigmoid(values)
    return sigmoid * (1.0 + values * (1.0 - sigmoid))


def contract(left, right, left_dim, right_dim):
    return lax.dot_general(
        left,
        right,
        (((left_dim,), (right_dim,)), ((), ())),
        preferred_element_type=jnp.float32,
    )


def normalize(retrieved, norm_gain):
    mean_square = jnp.mean(retrieved * retrieved, axis=-1, keepdims=True)
    return (retrieved * lax.rsqrt(mean_square + epsilon) * norm_gain).astype(jnp.bfloat16)


def narrow(x):
    return x.astype(jnp.bfloat16)


def paired(left, right):
    depth, width = right.shape
    left, right = (a.reshape(depth, width // HEAD_DIM, HEAD_DIM) for a in (left, right))
    return jnp.concatenate([left, right], axis=2).reshape(depth, 2 * width)


def shards(
    tokens,
    mem_query_w,
    mem_key_w,
    mem_value_w,
    mem_in,
    mem_out,
    forget_levels,
    momentum_levels,
    step_levels,
    plan,
    norm_gain,
    attn_query_w,
    attn_key_w,
    attn_value_w,
    attn_out_w,
):
    tok_rows, width = tokens.shape
    n_seq = lax.axis_size("seq")
    my_seq = lax.axis_index("seq")
    hidden_units = mem_out.shape[0]
    share = hidden_units // n_seq
    key_part = narrow(contract(tokens, mem_key_w, 1, 0))
    mem_key = gather(key_part, "head", 1, 0)
    mem_query = lax.all_gather(
        narrow(contract(tokens, mem_query_w, 1, 0)), "head", axis=1, tiled=True
    )
    value_part = narrow(contract(tokens, mem_value_w, 1, 0)).astype(jnp.float32)
    plan_all = lax.all_gather(plan, "seq", axis=0, tiled=True)

    in_turned = mem_in.T
    out_narrow = narrow(mem_out)
    pre_act = contract(mem_key, narrow(mem_in), 1, 0)
    hidden = narrow(jax.nn.silu(pre_act))
    predicted = scatter_sum(narrow(contract(hidden, out_narrow, 1, 0)), "head", 1, 1)
    residual_err = gather(narrow(2.0 / tok_rows * (predicted - value_part)), "head", 1, 2)
    grad_out = contract(hidden, residual_err, 0, 0)
    slope_term = narrow(contract(residual_err, out_narrow, 1, 1) * silu_slope(pre_act))
    grad_in = contract(slope_term, mem_key, 0, 0)
    grads = narrow(jnp.concatenate([grad_in, grad_out], axis=1)).reshape(
        n_seq, share, 2 * width
    )

    def mine(array, dim):
        return lax.dynamic_slice_in_dim(array, my_seq * share, share, dim)

    first = jnp.concatenate([mine(in_turned, 0), mine(mem_out, 0)], axis=1)
    matches = plan_all[:, None] == jnp.arange(forget_levels.shape[0], dtype=jnp.int32)[None, :]

    def gate(table):
        chosen = jnp.sum(jnp.where(matches[:, :, None], mine(table, 1)[None], 0.0), axis=1)
        return jnp.broadcast_to(chosen[:, :, None], (n_seq, share, 128))

    weights = evolve(
        grads, first, gate(forget_levels), gate(momentum_levels), gate(step_levels), 3
    ).reshape(hidden_units, 2 * width)
    query_hidden = narrow(jax.nn.silu(contract(mem_query, weights[:, :width], 1, 1)))
    retrieved = scatter_sum(
        narrow(contract(query_hidden, weights[:, width:], 1, 0)), "head", 0, 4
    )
    normed = gather(normalize(retrieved, norm_gain), "head", 0, 5)
    query_w = paired(attn_query_w, jnp.zeros_like(attn_query_w))
    pair_w = paired(attn_key_w, attn_value_w)
    att_query = narrow(contract(normed, query_w, 1, 0))
    att_pairs = narrow(contract(normed, pair_w, 1, 0))
    context = attend(att_query, att_pairs, 6)
    heads = attn_out_w.shape[0] // HEAD_DIM
    out_rows = attn_out_w.reshape(heads, HEAD_DIM, width)
    out_w = jnp.concatenate([jnp.zeros_like(out_rows), out_rows], axis=1).reshape(
        heads * LANES, width
    )
    return narrow(scatter_sum(narrow(contract(context, out_w, 1, 0)), "head", 1, 7))


def solution(mesh):
    in_specs = (
        P("seq", None),
        P(None, "head"),
        P(None, "head"),
        P(None, "head"),
        P(None, "head"),
        P("head", None),
        P(None, "head"),
        P(None, "head"),
        P(None, "head"),
        P("seq"),
        P(),
        P(None, "head"),
        P(None, "head"),
        P(None, "head"),
        P("head", None),
    )
    out_specs = P("seq", "head")
    return jax.shard_map(shards, mesh=mesh, in_specs=in_specs, out_specs=out_specs, check_vma=False)
```

time: 1020 us -> 399 us (0.39)
  waiting for transfers between devices: 642 us -> 0.02 us
  Pallas kernels: 0 us -> 316 us
  other arithmetic: 149 us -> 12.2 us
  matrix products: 114 us -> 32.2 us
  blocking collectives: 38.4 us -> 5.61 us
  starting transfers between devices: 22.1 us -> 0.01 us
  local copies, waits for them, and re-layouts: 34.1 us -> 18.3 us
    all_gather x7 -> x1, waiting for transfers between devices: 376 us -> 0.01 us  [shards(): lax.all_gather(narrow(contract(tokens, mem_query_w, 1, 0)), 'head', axis=...]
    pallas_call x0 -> x8, Pallas kernels: none -> 316 us  [the longest x1 109 us: evolve(): pl.pallas_call(functools.partial(memory_kernel, n), out_shape=jax.ShapeDt...]
    ppermute x16 -> x0, waiting for transfers between devices: 159 us -> none  [shifted(): return lax.ppermute(value, axis, pairs)]
    add x31 -> x0, other arithmetic: 131 us -> none  [the longest x15 83 us: compose(): as_rows(after_cross) * prior_speed_out]
    reduce_scatter x3 -> x0, waiting for transfers between devices: 106 us -> none  [the longest x1 40 us: shards(): lax.psum_scatter(partial_out.astype(jnp.bfloat16), 'head', scatter_dimens...]
    dot_general x30 -> x11, matrix products: 114 us -> 32.2 us  [contract(): lax.dot_general(left, right, (((left_dim,), (right_dim,)), ((), ())), pre...]
    all_gather x2 -> x0, blocking collectives: 38.4 us -> none  [entering_2(): gathered = jax.tree.map(lambda a: lax.all_gather(a, axis), part)]
    ppermute x16 -> x0, starting transfers between devices: 21.2 us -> none  [shifted(): return lax.ppermute(value, axis, pairs)]
  transfers between devices with their start and end apart: 26 -> 1, of which waited for: 13 -> 0; matrix products, arithmetic and copies ran while one was open for 21% -> 10% of each run, Pallas kernels for 0% -> 41%
where the time goes in v1:
time: 399 us
  Pallas kernels  316 us (79%)
  matrix products  32.2 us (8%)
  local copies, waits for them, and re-layouts  18.3 us (5%)
  between operations  14.3 us (4%)
  other arithmetic  12.2 us (3%)
  blocking collectives  5.61 us (1%)
    pallas_call x1, Pallas kernels, evolve(): pl.pallas_call(functools.partial(memory_kernel, n), out_shape=jax.ShapeDt...  109 us
    pallas_call x6, Pallas kernels, comm_call(): pl.pallas_call(kernel, out_shape=out, in_specs=[ANY], out_specs=ANY, scra...  107 us
    pallas_call x1, Pallas kernels, attend(): pl.pallas_call(functools.partial(attention_kernel, n, heads), out_shape=j...  100 us
    dot_general x11, matrix products, contract(): lax.dot_general(left, right, (((left_dim,), (right_dim,)), ((), ())), pre...  32.2 us
    unnamed x39, local copies, waits for them, and re-layouts  9.11 us
  transfers between devices with their start and end apart: 1, of which 0 were waited for; matrix products, arithmetic and copies ran while one was open for 10% of the time, Pallas kernels for 41%

profile of v1, /device:TPU:27, one launch (start us, length us, event | category | flops | bytes accessed | tf_op | source)
XLA Modules:
  0.0 398.7 jit_solution(12122951838753189833)
XLA Ops:
  7.8 2.7 convolution_convert_fusion.9
  12.5 5.6 %all-reduce.2 = s32[16]{0:T(128)S(1)} all-reduce(s32[16]{0:T(128)S(1)} %dynamic-update-slice), channel_id=1, replica_groups=mesh['seq'=16,'head'=2] {'seq'}, use_global_device_ids=true, to_apply=%add.2 | all-reduce | flops 16 | bytes 128
  22.2 2.7 convolution_convert_fusion.8.x_ref
  24.9 18.2 %shard_map.145 = bf16[512,1024]{1,0:T(8,128)(2,1)} custom-call(bf16[512,512]{1,0:T(8,128)(2,1)} %convolution_convert_fusion.8.x_ref), custom_call_target="tpu_custom_call" | custom-call | tf_op jit(solution)/shard_map/pallas_call | solution.py:87
  43.2 2.1 fusion.16
  46.2 1.7 convolution_convert_fusion.6.x_ref
  48.0 17.2 %shard_map.146 = bf16[2,512,512]{2,1,0:T(8,128)(2,1)} custom-call(bf16[512,1024]{1,0:T(8,128)(2,1)} %convolution_convert_fusion.6.x_ref), custom_call_target="tpu_custom_call" | custom-call | tf_op jit(solution)/shard_map/pallas_call | solution.py:87
  68.2 18.2 %shard_map.147 = bf16[512,1024]{1,0:T(8,128)(2,1)} custom-call(bf16[512,512]{1,0:T(8,128)(2,1)} %fusion.4.x_ref), custom_call_target="tpu_custom_call" | custom-call | tf_op jit(solution)/shard_map/pallas_call | solution.py:87
  86.5 3.1 convolution_convert_fusion.4
  90.1 2.3 copy.24
  95.5 1.6 concatenate.27
  98.8 4.7 %convolution_convert_fusion.5 = bf16[512,1024]{1,0:T(8,128)(2,1)} fusion(bf16[512,1024]{1,0:T(8,128)(2,1)S(1)} %copy-done.2, bf16[512,1024]{1,0:T(8,128)(2,1)} %shard_map.147, f32[512,512]{1,0:T(8,128)} %copy-done.10, f32[512,1024]{1,0:T(8,128)} %param.20), kind=kOutput, calls=%fused_computation.9 | convolution fusion | flops 1077149696 | bytes 6291456 | tf_op jit(solution)/shard_map/dot_general | solution.py:373
  103.5 3.1 pad_maximum_fusion.grads_ref
  109.1 109.2 %shard_map.148 = bf16[16,32,2048]{2,1,0:T(8,128)(2,1)} custom-call(bf16[16,32,2048]{2,1,0:T(8,128)(2,1)} %pad_maximum_fusion.grads_ref, f32[32,2048]{1,0:T(8,128)} %pad_maximum_fusion.2.first_ref, f32[16,32,128]{2,1,0:T(8,128)} %broadcast_in_dim.70.forget_ref, f32[16,32,128]{2,1,0:T(8,128)} %broadcast_in_dim.72.momentum_ref, ...), custom_call_target="tpu_custom_call" | custom-call | tf_op jit(solution)/shard_map/pallas_call | solution.py:169
  218.3 1.6 pad_maximum_fusion.1
  220.0 4.3 %convolution_convert_fusion.3.x_ref = bf16[512,1024]{1,0:T(8,128)(2,1)} fusion(bf16[512,2048]{1,0:T(8,128)(2,1)} %bitcast.35, bf16[512,1024]{1,0:T(8,128)(2,1)} %all-gather.2.cloned.1.call-done), kind=kOutput, calls=%fused_computation.7 | convolution fusion | flops 1075576832 | bytes 4194304 | tf_op jit(solution)/shard_map/dot_general | solution.py:373
  224.2 17.2 %shard_map.149 = bf16[2,256,1024]{2,1,0:T(8,128)(2,1)} custom-call(bf16[512,1024]{1,0:T(8,128)(2,1)} %convolution_convert_fusion.3.x_ref), custom_call_target="tpu_custom_call" | custom-call | tf_op jit(solution)/shard_map/pallas_call | solution.py:87
  244.2 18.2 %shard_map.150 = bf16[512,1024]{1,0:T(8,128)(2,1)} custom-call(bf16[256,1024]{1,0:T(8,128)(2,1)} %multiply_convert_fusion.x_ref), custom_call_target="tpu_custom_call" | custom-call | tf_op jit(solution)/shard_map/pallas_call | solution.py:87
  262.4 3.6 convolution_convert_fusion.1.kv_ref
  266.1 2.3 convolution_convert_fusion.2.q_ref
  268.4 100.3 %shard_map.151 = bf16[512,1024]{1,0:T(8,128)(2,1)} custom-call(bf16[512,1024]{1,0:T(8,128)(2,1)} %convolution_convert_fusion.2.q_ref, bf16[512,1024]{1,0:T(8,128)(2,1)} %convolution_convert_fusion.1.kv_ref), custom_call_target="tpu_custom_call" | custom-call | tf_op jit(solution)/shard_map/pallas_call | solution.py:346
  368.7 3.5 convolution_convert_fusion.x_ref
  372.2 17.3 %shard_map.152 = bf16[2,512,512]{2,1,0:T(8,128)(2,1)} custom-call(bf16[512,1024]{1,0:T(8,128)(2,1)} %convolution_convert_fusion.x_ref), custom_call_target="tpu_custom_call" | custom-call | tf_op jit(solution)/shard_map/pallas_call | solution.py:87
  389.5 2.3 reduce_sum.72
  (58 shorter events, 21.1 us)
Async XLA Ops:
  6.5 1.2 copy-start
  6.5 4.6 %copy-start.15 = (u32[32]{0:T(128)S(1)}, u32[32]{0:T(128)}, u32[]{:S(2)}) copy-start(u32[32]{0:T(128)} %constant.37) | copy-start | bytes 388
  6.5 12.4 %copy-start.3 = (f32[1024,512]{1,0:T(8,128)S(1)}, f32[1024,512]{1,0:T(8,128)}, u32[]{:S(2)}) copy-start(f32[1024,512]{1,0:T(8,128)} %param.19) | copy-start | bytes 6291460
  6.5 213.4 %all-gather.2.cloned.1.call-start = ((), (), s32[]{:S(2)}) async-start(), calls=%async_computation | async-start | bytes 1572864 | tf_op jit(solution)/shard_map/all_gather | solution.py:420
  43.1 3.1 copy-start.12
  45.2 1.0 copy-start.10
  48.0 18.8 %copy-start.14 = (bf16[1024,512]{1,0:T(8,128)(2,1)S(1)}, bf16[1024,512]{1,0:T(8,128)(2,1)}, u32[]{:S(2)}) copy-start(bf16[1024,512]{1,0:T(8,128)(2,1)} %param.18) | copy-start | bytes 3145732
  66.7 19.8 %copy-start.11 = (f32[512,512]{1,0:T(8,128)S(1)}, f32[512,512]{1,0:T(8,128)}, u32[]{:S(2)}) copy-start(f32[512,512]{1,0:T(8,128)} %copy-done.10) | copy-start | bytes 3145732
  86.5 3.1 copy-start.8
  93.9 1.6 copy-start.9
  95.5 3.3 copy-start.2
  109.1 109.2 %copy-start.1 = (bf16[1024,512]{0,1:T(8,128)(2,1)S(1)}, bf16[1024,512]{0,1:T(8,128)(2,1)}, u32[]{:S(2)}) copy-start(bf16[1024,512]{0,1:T(8,128)(2,1)} %copy.24) | copy-start | bytes 3145732
  241.5 1.7 copy-start.13
  243.0 19.4 %copy-start.6 = (bf16[1024,8,128]{0,2,1:T(8,128)(2,1)S(1)}, bf16[1024,8,128]{0,2,1:T(8,128)(2,1)}, u32[]{:S(2)}) copy-start(bf16[1024,8,128]{0,2,1:T(8,128)(2,1)} %pad_maximum_fusion.1) | copy-start | bytes 6291460
  262.4 3.7 copy-start.5
  262.4 3.7 copy-start.7
  268.4 100.3 %copy-start.4 = (bf16[8,128,1024]{2,1,0:T(8,128)(2,1)S(1)}, bf16[8,128,1024]{2,1,0:T(8,128)(2,1)}, u32[]{:S(2)}) copy-start(bf16[8,128,1024]{2,1,0:T(8,128)(2,1)} %concatenate.27) | copy-start | bytes 6291460
Sparse Core Ops, SparseCore 0:
  10.6 25.5 all-gather.1

commit v2 on v1

--- a/solution.py
+++ b/solution.py
@@ -115,25 +115,42 @@
     return jnp.sum(parts.astype(jnp.float32), axis=0)
 
 
+def whole_sum(x, axis, identity):
+    parts = gather(x, axis, 0, identity).reshape(-1, *x.shape)
+    return jnp.sum(parts.astype(jnp.float32), axis=0)
+
+
 def memory_kernel(
-    n, grads_ref, first_ref, forget_ref, momentum_ref, rate_ref, o_ref,
-    came, stage, send, recv, send_back, recv_back, local, local_back,
+    n, grads_ref, gates_ref, first_ref, o_ref,
+    came, gates, wide, stage, send, recv, send_gate, recv_gate, send_back, recv_back, local,
 ):
     me = lax.axis_index("seq")
     meet("seq", n)
     copies = []
     for k in range(1, n):
         peer = lax.rem(me + k, n)
+        gate_copy = remote(
+            gates_ref.at[peer], gates.at[me], send_gate.at[k - 1], recv_gate.at[k - 1], "seq", peer
+        )
+        gate_copy.start()
         copy = remote(
             grads_ref.at[peer], came.at[me], send.at[k - 1], recv.at[k - 1], "seq", peer
         )
         copy.start()
-        copies.append(copy)
-    own = pltpu.make_async_copy(grads_ref.at[me], came.at[me], local)
+        copies += [gate_copy, copy]
+    own_gates = pltpu.make_async_copy(gates_ref.at[me], gates.at[me], local.at[0])
+    own_gates.start()
+    own = pltpu.make_async_copy(grads_ref.at[me], came.at[me], local.at[1])
     own.start()
+    own_gates.wait()
     own.wait()
     for copy in copies:
         copy.wait()
+
+    for g in range(n):
+        row = gates[g]
+        for which in range(3):
+            wide[which, g] = jnp.broadcast_to(row[:, which : which + 1], row.shape)
 
     def columns(c, carry):
         window = pl.ds(pl.multiple_of(c * 128, 128), 128)
@@ -143,8 +160,8 @@
             stage[g, :, window] = weight.astype(jnp.bfloat16)
             if g < n - 1:
                 grad = came[g, :, window].astype(jnp.float32)
-                speed = momentum_ref[g] * speed - rate_ref[g] * grad
-                weight = (1.0 - forget_ref[g]) * weight + speed
+                speed = wide[0, g] * speed - wide[2, g] * grad
+                weight = (1.0 - wide[1, g]) * weight + speed
         return carry
 
     lax.fori_loop(0, first_ref.shape[1] // 128, columns, 0)
@@ -157,37 +174,35 @@
         )
         copy.start()
         copies.append(copy)
-    own = pltpu.make_async_copy(stage.at[me], o_ref.at[me], local_back)
+    own = pltpu.make_async_copy(stage.at[me], o_ref.at[me], local.at[2])
     own.start()
     own.wait()
     for copy in copies:
         copy.wait()
 
 
-def evolve(grads, first, forget, momentum, rate, identity):
+def evolve(grads, gates, first, identity):
     n = grads.shape[0]
     return pl.pallas_call(
         functools.partial(memory_kernel, n),
         out_shape=jax.ShapeDtypeStruct(grads.shape, jnp.bfloat16),
-        in_specs=[ANY, VMEM, VMEM, VMEM, VMEM],
+        in_specs=[ANY, ANY, VMEM],
         out_specs=ANY,
         scratch_shapes=[
             pltpu.VMEM(grads.shape, jnp.bfloat16),
+            pltpu.VMEM(gates.shape, jnp.float32),
+            pltpu.VMEM((3, *gates.shape), jnp.float32),
             pltpu.VMEM(grads.shape, jnp.bfloat16),
-            pltpu.SemaphoreType.DMA((n - 1,)),
-            pltpu.SemaphoreType.DMA((n - 1,)),
-            pltpu.SemaphoreType.DMA((n - 1,)),
-            pltpu.SemaphoreType.DMA((n - 1,)),
-            pltpu.SemaphoreType.DMA,
-            pltpu.SemaphoreType.DMA,
+            *[pltpu.SemaphoreType.DMA((n - 1,))] * 6,
+            pltpu.SemaphoreType.DMA((3,)),
         ],
         compiler_params=pltpu.CompilerParams(collective_id=identity, has_side_effects=True),
-    )(grads, first, forget, momentum, rate)
+    )(grads, gates, first)
 
 
 def attention_kernel(
     n, heads, q_ref, kv_ref, o_ref,
-    q_all, kv_all, ctx, q_send, q_recv, kv_send, kv_recv, ctx_send, ctx_recv, local,
+    q_all, kv_all, ctx, peaks, totals, q_send, q_recv, kv_send, kv_recv, ctx_send, ctx_recv, local,
 ):
     me = lax.axis_index("seq")
     chunk = me // heads
@@ -246,9 +261,6 @@
                 kv_all.at[slot], kv_all.at[slot], kv_send.at[0], kv_recv.at[slot], "seq", other
             ).wait_recv()
 
-    for slot in range(SPAN):
-        await_kv(slot)
-
     row = lax.broadcasted_iota(jnp.int32, (rows, rows), 0)
     column = lax.broadcasted_iota(jnp.int32, (rows, rows), 1)
     scale = math.log2(math.e) * HEAD_DIM**-0.5
@@ -277,7 +289,7 @@
             chunk * heads + tile,
         )
 
-    def one_tile(tile, carry):
+    def near(tile, carry):
         @pl.when(tile != my_tile)
         def _():
             remote(
@@ -286,7 +298,6 @@
 
         await_kv(tile + SPAN)
         query = q_all[tile]
-        block = chunk * heads + tile
         scores, values = scored(query, tile + SPAN)
         scores = jnp.where(column <= row, scores, -1e30)
         peak = jnp.max(scores, axis=1, keepdims=True)
@@ -297,7 +308,31 @@
             scores, values = scored(query, tile + SPAN - back)
             return absorb(state, scores, values)
 
-        state = lax.fori_loop(1, jnp.minimum(block, SPAN - 1) + 1, whole, state)
+        peak, total = lax.fori_loop(1, jnp.minimum(tile, SPAN - 1) + 1, whole, state)
+        peaks[tile] = peak
+        totals[tile] = total
+        return carry
+
+    def far(step, carry):
+        tile = heads - 1 - step
+        block = chunk * heads + tile
+
+        @pl.when(tile < SPAN)
+        def _():
+            await_kv(tile)
+
+        query = q_all[tile]
+
+        def whole(back, state):
+            scores, values = scored(query, tile + SPAN - back)
+            return absorb(state, scores, values)
+
+        state = lax.fori_loop(
+            jnp.minimum(tile, SPAN - 1) + 1,
+            jnp.minimum(block, SPAN - 1) + 1,
+            whole,
+            (peaks[tile], totals[tile]),
+        )
 
         def oldest(back, state):
             scores, values = scored(query, tile)
@@ -316,7 +351,10 @@
 
         return carry
 
-    lax.fori_loop(0, heads, one_tile, 0)
+    lax.fori_loop(0, heads, near, 0)
+    for slot in range(heads, SPAN):
+        await_kv(slot)
+    lax.fori_loop(0, heads, far, 0)
 
     pltpu.make_async_copy(ctx.at[my_tile], lanes(o_ref, head), local.at[2]).wait()
     for tile in range(heads):
@@ -352,6 +390,8 @@
             pltpu.VMEM((heads, rows, LANES), jnp.bfloat16),
             pltpu.VMEM((SPAN + heads, rows, LANES), jnp.bfloat16),
             pltpu.VMEM((heads, rows, LANES), jnp.bfloat16),
+            pltpu.VMEM((heads, rows, 1), jnp.float32),
+            pltpu.VMEM((heads, rows, LANES), jnp.float32),
             pltpu.SemaphoreType.DMA((n - 1,)),
             pltpu.SemaphoreType.DMA((heads,)),
             pltpu.SemaphoreType.DMA((n - 1,)),
@@ -421,14 +461,20 @@
         narrow(contract(tokens, mem_query_w, 1, 0)), "head", axis=1, tiled=True
     )
     value_part = narrow(contract(tokens, mem_value_w, 1, 0)).astype(jnp.float32)
-    plan_all = lax.all_gather(plan, "seq", axis=0, tiled=True)
-
-    in_turned = mem_in.T
+    pair = lax.axis_size("head") <= 2
     out_narrow = narrow(mem_out)
     pre_act = contract(mem_key, narrow(mem_in), 1, 0)
     hidden = narrow(jax.nn.silu(pre_act))
-    predicted = scatter_sum(narrow(contract(hidden, out_narrow, 1, 0)), "head", 1, 1)
-    residual_err = gather(narrow(2.0 / tok_rows * (predicted - value_part)), "head", 1, 2)
+    partial = contract(hidden, out_narrow, 1, 0)
+    if pair:
+        mine_first = lax.axis_index("head") * value_part.shape[1]
+        value_wide = lax.dynamic_update_slice_in_dim(
+            jnp.zeros_like(partial), value_part, mine_first, 1
+        )
+        residual_err = narrow(2.0 / tok_rows * whole_sum(narrow(partial - value_wide), "head", 1))
+    else:
+        predicted = scatter_sum(narrow(partial), "head", 1, 1)
+        residual_err = gather(narrow(2.0 / tok_rows * (predicted - value_part)), "head", 1, 2)
     grad_out = contract(hidden, residual_err, 0, 0)
     slope_term = narrow(contract(residual_err, out_narrow, 1, 1) * silu_slope(pre_act))
     grad_in = contract(slope_term, mem_key, 0, 0)
@@ -439,21 +485,21 @@
     def mine(array, dim):
         return lax.dynamic_slice_in_dim(array, my_seq * share, share, dim)
 
-    first = jnp.concatenate([mine(in_turned, 0), mine(mem_out, 0)], axis=1)
-    matches = plan_all[:, None] == jnp.arange(forget_levels.shape[0], dtype=jnp.int32)[None, :]
-
-    def gate(table):
-        chosen = jnp.sum(jnp.where(matches[:, :, None], mine(table, 1)[None], 0.0), axis=1)
-        return jnp.broadcast_to(chosen[:, :, None], (n_seq, share, 128))
-
-    weights = evolve(
-        grads, first, gate(forget_levels), gate(momentum_levels), gate(step_levels), 3
-    ).reshape(hidden_units, 2 * width)
+    first = jnp.concatenate([mine(mem_in, 1).T, mine(mem_out, 0)], axis=1)
+    matches = jnp.arange(forget_levels.shape[0], dtype=jnp.int32)[:, None] == plan[0]
+    chosen = [
+        jnp.sum(jnp.where(matches, table, 0.0), axis=0)
+        for table in (momentum_levels, forget_levels, step_levels)
+    ]
+    gates = jnp.pad(jnp.stack(chosen, axis=1), ((0, 0), (0, 125))).reshape(n_seq, share, 128)
+    weights = evolve(grads, gates, first, 3).reshape(hidden_units, 2 * width)
     query_hidden = narrow(jax.nn.silu(contract(mem_query, weights[:, :width], 1, 1)))
-    retrieved = scatter_sum(
-        narrow(contract(query_hidden, weights[:, width:], 1, 0)), "head", 0, 4
-    )
-    normed = gather(normalize(retrieved, norm_gain), "head", 0, 5)
+    partial = narrow(contract(query_hidden, weights[:, width:], 1, 0))
+    if pair:
+        normed = normalize(whole_sum(partial, "head", 4), norm_gain)
+    else:
+        retrieved = scatter_sum(partial, "head", 0, 4)
+        normed = gather(normalize(retrieved, norm_gain), "head", 0, 5)
     query_w = paired(attn_query_w, jnp.zeros_like(attn_query_w))
     pair_w = paired(attn_key_w, attn_value_w)
     att_query = narrow(contract(normed, query_w, 1, 0))

time: 399 us -> 398 us (level)
  blocking collectives: 5.61 us -> 0 us
  Pallas kernels: 316 us -> 320 us
    unnamed x1 -> x0, blocking collectives: 5.61 us -> none
    reduce_sum x1 -> x3, other arithmetic: 0.15 us -> 4.73 us  [the longest x2 4.63 us: whole_sum(): return jnp.sum(parts.astype(jnp.float32), axis=0)]
    pallas_call x1, Pallas kernels: 109 us -> 114 us  [evolve(): pl.pallas_call(functools.partial(memory_kernel, n), out_shape=jax.ShapeDt...]
    pallas_call x6 -> x4, Pallas kernels: 107 us -> 104 us  [comm_call(): pl.pallas_call(kernel, out_shape=out, in_specs=[ANY], out_specs=ANY, scra...]
    unnamed x39 -> x41, local copies, waits for them, and re-layouts: 9.11 us -> 10.7 us
  transfers between devices with their start and end apart: 1 -> 1, of which waited for: 0 -> 0; matrix products, arithmetic and copies ran while one was open for 10% -> 9% of each run, Pallas kernels for 41% -> 42%
where the time goes in v2:
time: 398 us; the launch traced here: 394 us
  Pallas kernels  320 us (80%)
  matrix products  30.1 us (8%)
  local copies, waits for them, and re-layouts  16.8 us (4%)
  between operations  14.4 us (4%)
  other arithmetic  12.8 us (3%)
    pallas_call x1, Pallas kernels, evolve(): pl.pallas_call(functools.partial(memory_kernel, n), out_shape=jax.ShapeDt...  114 us
    pallas_call x4, Pallas kernels, comm_call(): pl.pallas_call(kernel, out_shape=out, in_specs=[ANY], out_specs=ANY, scra...  104 us
    pallas_call x1, Pallas kernels, attend(): pl.pallas_call(functools.partial(attention_kernel, n, heads), out_shape=j...  102 us
    dot_general x11, matrix products, contract(): lax.dot_general(left, right, (((left_dim,), (right_dim,)), ((), ())), pre...  30.1 us
    unnamed x41, local copies, waits for them, and re-layouts  10.7 us
  transfers between devices with their start and end apart: 1, of which 0 were waited for; matrix products, arithmetic and copies ran while one was open for 9% of the time, Pallas kernels for 42%

profile of v2, /device:TPU:27, one launch (start us, length us, event | category | flops | bytes accessed | tf_op | source)
XLA Modules:
  0.0 394.1 jit_solution(7765813760327539956)
XLA Ops:
  7.8 2.8 convolution_convert_fusion.8
  10.6 2.9 convolution_convert_fusion.7.x_ref
  13.4 18.2 %shard_map.145 = bf16[512,1024]{1,0:T(8,128)(2,1)} custom-call(bf16[512,512]{1,0:T(8,128)(2,1)} %convolution_convert_fusion.7.x_ref), custom_call_target="tpu_custom_call" | custom-call | tf_op jit(solution)/shard_map/pallas_call | solution.py:87
  31.7 2.9 fusion.14
  39.7 1.7 subtract_convert_fusion.x_ref
  41.4 34.7 %shard_map.146 = bf16[1024,1024]{1,0:T(8,128)(2,1)} custom-call(bf16[512,1024]{1,0:T(8,128)(2,1)} %subtract_convert_fusion.x_ref), custom_call_target="tpu_custom_call" | custom-call | tf_op jit(solution)/shard_map/pallas_call | solution.py:87
  76.1 2.3 convert_reduce_fusion.1
  79.8 1.8 convolution_convert_fusion.4
  84.8 2.3 copy.26
  88.5 1.6 concatenate.25
  90.1 1.6 concatenate.27
  91.7 5.0 %convolution_convert_fusion.5 = bf16[512,1024]{1,0:T(8,128)(2,1)} fusion(bf16[512,1024]{1,0:T(8,128)(2,1)S(1)} %copy-done.1, f32[512,512]{1,0:T(8,128)} %fusion.14, f32[512,1024]{1,0:T(8,128)} %param.20, f32[512,1024]{1,0:T(8,128)} %copy-done.5), kind=kOutput, calls=%fused_computation.13 | convolution fusion | flops 1078198272 | bytes 7340032 | tf_op jit(solution)/shard_map/dot_general | solution.py:413
  96.7 3.1 pad_maximum_fusion.grads_ref
  99.8 113.6 %shard_map.147 = bf16[16,32,2048]{2,1,0:T(8,128)(2,1)} custom-call(bf16[16,32,2048]{2,1,0:T(8,128)(2,1)} %pad_maximum_fusion.grads_ref, f32[16,32,128]{2,1,0:T(8,128)} %bitcast.43, f32[32,2048]{1,0:T(8,128)} %pad_maximum_fusion.2.first_ref), custom_call_target="tpu_custom_call" | custom-call | tf_op jit(solution)/shard_map/pallas_call | solution.py:186
  213.4 1.6 pad_maximum_fusion.1
  215.1 4.3 %convolution_convert_fusion.3.x_ref = bf16[512,1024]{1,0:T(8,128)(2,1)} fusion(bf16[512,2048]{1,0:T(8,128)(2,1)} %bitcast.42, bf16[512,1024]{1,0:T(8,128)(2,1)} %all-gather.2.cloned.1.call-done), kind=kOutput, calls=%fused_computation.11 | convolution fusion | flops 1075576832 | bytes 4194304 | tf_op jit(solution)/shard_map/dot_general | solution.py:413
  219.3 32.9 %shard_map.148 = bf16[1024,1024]{1,0:T(8,128)(2,1)} custom-call(bf16[512,1024]{1,0:T(8,128)(2,1)} %convolution_convert_fusion.3.x_ref), custom_call_target="tpu_custom_call" | custom-call | tf_op jit(solution)/shard_map/pallas_call | solution.py:87
  252.2 2.3 convert_reduce_fusion
  256.1 2.3 convolution_convert_fusion.1.kv_ref
  258.4 2.3 convolution_convert_fusion.2.q_ref
  260.7 102.2 %shard_map.149 = bf16[512,1024]{1,0:T(8,128)(2,1)} custom-call(bf16[512,1024]{1,0:T(8,128)(2,1)} %convolution_convert_fusion.2.q_ref, bf16[512,1024]{1,0:T(8,128)(2,1)} %convolution_convert_fusion.1.kv_ref), custom_call_target="tpu_custom_call" | custom-call | tf_op jit(solution)/shard_map/pallas_call | solution.py:384
  363.0 3.5 convolution_convert_fusion.x_ref
  366.4 18.5 %shard_map.150 = bf16[2,512,512]{2,1,0:T(8,128)(2,1)} custom-call(bf16[512,1024]{1,0:T(8,128)(2,1)} %convolution_convert_fusion.x_ref), custom_call_target="tpu_custom_call" | custom-call | tf_op jit(solution)/shard_map/pallas_call | solution.py:87
  384.9 2.3 reduce_sum.72
  (54 shorter events, 13.1 us)
Async XLA Ops:
  6.5 1.2 copy-start
  6.5 208.5 %all-gather.2.cloned.1.call-start = ((), (), s32[]{:S(2)}) async-start(), calls=%async_computation | async-start | bytes 1572864 | tf_op jit(solution)/shard_map/all_gather | solution.py:460
  10.6 21.1 %copy-start.3 = (f32[1024,512]{1,0:T(8,128)S(1)}, f32[1024,512]{1,0:T(8,128)}, u32[]{:S(2)}) copy-start(f32[1024,512]{1,0:T(8,128)} %param.19) | copy-start | bytes 6291460
  36.6 1.2 copy-start.16
  37.8 1.2 copy-start.11
  37.8 1.9 copy-start.15
  78.4 1.3 copy-start.5
  79.8 1.8 copy-start.8
  79.8 3.5 copy-start.12
  79.8 3.5 copy-start.13
  79.8 3.5 copy-start.14
  81.6 2.7 copy-start.9
  88.5 1.6 copy-start.10
  90.1 1.6 copy-start.1
  99.8 113.6 %copy-start.2 = (bf16[1024,512]{0,1:T(8,128)(2,1)S(1)}, bf16[1024,512]{0,1:T(8,128)(2,1)}, u32[]{:S(2)}) copy-start(bf16[1024,512]{0,1:T(8,128)(2,1)} %copy.26) | copy-start | bytes 3145732
  254.5 1.6 copy-start.7
  254.6 1.6 copy-start.17
  256.1 2.3 copy-start.6
  260.7 102.2 %copy-start.4 = (bf16[8,128,1024]{2,1,0:T(8,128)(2,1)S(1)}, bf16[8,128,1024]{2,1,0:T(8,128)(2,1)}, u32[]{:S(2)}) copy-start(bf16[8,128,1024]{2,1,0:T(8,128)(2,1)} %concatenate.27) | copy-start | bytes 6291460
Sparse Core Ops, SparseCore 0:
  10.7 28.2 all-gather.1
